TPU v7x, 32 devices: a whole 2x2x4 slice. The times are simulated.
32 devices in a mesh: group: 4 (over z), batch: 8 (over y, x, core).
Axes of the slice: x: 2, y: 2, z: 4, core: 2. Of those that a mesh axis runs over, the one named last changes fastest.
Arguments:
- embeds: bfloat16 [65536, 256], P(('group', 'batch')), may hold values from -6 to 6
- out_grad: bfloat16 [65536, 256], P(('group', 'batch')), may hold values from -48 to 48
- w_query: bfloat16 [256, 256], replicated, may hold values from -0.375 to 0.375
- w_key: bfloat16 [256, 256], replicated, may hold values from -0.375 to 0.375
- w_value: bfloat16 [256, 256], replicated, may hold values from -0.375 to 0.375
- lengths: int32 [128], P(('group', 'batch')), may hold values from 1 to 512, as said below
- item_rows: int32 [65536], P(('group', 'batch')), may hold values from 0 to 2047, as said below
- tile_owner: int32 [512], P(('group', 'batch')), may hold values from 0 to 3, as said below
Outputs:
- table_grad: float32 [8192, 256], P(('group', 'batch'))
Inputs may be any that keep to these rules, and one draw needn't show every extreme that they name: `lengths`: a history's live tokens are its first positions; in every draw some history has exactly 512 live tokens. `tile_owner`: among the first 8 tiles of each device's own tiles, and among the last 8, every group owns exactly 2 tiles. `item_rows`: of the 128 tokens of each tile, at most 32 have rows r with the same r // 256, and in every tile some value of r // 256 is taken by exactly 32 tokens.
All inputs are finite; a program needn't handle non-finite values.
Results may differ from a plain program's by a relative error of at most 0.0024.
The roundings to bfloat16 on the way count: a program that leaves them out, or rounds other values in their place, can miss the bound.
Values may be sent and summed in bfloat16 or wider, within the bound.
No kernel may reach another device: no remote copies, remote signals or barrier semaphores. Data moves between devices by JAX's collectives and lax.ppermute only.
A program may use at most 64 MiB of HBM per device.

v0:
```python
import math
import jax
import jax.numpy as jnp
from jax import lax
from jax.sharding import PartitionSpec as P

HEADS = 2
TILE = 128
SEQ_LEN = 512
ROWS_DEV = 256


def sequence_grads(query, key_rows, value, grad_out, count, w_query, w_key, w_value):
    span = query.shape[0]
    position = lax.broadcasted_iota(jnp.int32, (span, span), 0)
    other = lax.broadcasted_iota(jnp.int32, (span, span), 1)
    live = ((other <= position) & (position < count)).astype(jnp.float32)
    weight = live / count.astype(jnp.float32)
    scale = 1.0 / math.sqrt(query.shape[2])
    scores = jnp.einsum("ihd,jhd->hij", query, key_rows, preferred_element_type=jnp.float32) * scale
    sigma = jax.nn.sigmoid(scores)
    attend = (scores * sigma * weight).astype(jnp.bfloat16)
    value_grad = jnp.einsum(
        "hij,ihd->jhd", attend, grad_out, preferred_element_type=jnp.float32
    ).astype(jnp.bfloat16)
    attend_grad = jnp.einsum("ihd,jhd->hij", grad_out, value, preferred_element_type=jnp.float32)
    score_grad = (attend_grad * weight * sigma * (1.0 + scores * (1.0 - sigma))).astype(
        jnp.bfloat16
    )
    query_grad = (
        jnp.einsum("hij,jhd->ihd", score_grad, key_rows, preferred_element_type=jnp.float32) * scale
    ).astype(jnp.bfloat16)
    key_grad = (
        jnp.einsum("hij,ihd->jhd", score_grad, query, preferred_element_type=jnp.float32) * scale
    ).astype(jnp.bfloat16)
    width = w_query.shape[0]
    token = jnp.dot(query_grad.reshape(span, width), w_query.T, preferred_element_type=jnp.float32)
    token = token + jnp.dot(
        key_grad.reshape(span, width), w_key.T, preferred_element_type=jnp.float32
    )
    token = token + jnp.dot(
        value_grad.reshape(span, width), w_value.T, preferred_element_type=jnp.float32
    )
    return token.astype(jnp.bfloat16)


def token_grads(embeds, out_grad, w_query, w_key, w_value, lengths):
    history_count = lengths.shape[0]
    width = embeds.shape[1]
    head_size = width // HEADS

    def project(weight_matrix):
        return (
            jnp.dot(embeds, weight_matrix, preferred_element_type=jnp.float32)
            .astype(jnp.bfloat16)
            .reshape(history_count, SEQ_LEN, HEADS, head_size)
        )

    query = project(w_query)
    key_rows = project(w_key)
    value = project(w_value)
    grad_heads = out_grad.reshape(history_count, SEQ_LEN, HEADS, head_size)
    half_span = SEQ_LEN // 2

    def short_history(item):
        front = sequence_grads(
            item[0][:half_span],
            item[1][:half_span],
            item[2][:half_span],
            item[3][:half_span],
            item[4],
            w_query,
            w_key,
            w_value,
        )
        return jnp.concatenate(
            [front, jnp.zeros((SEQ_LEN - half_span, width), jnp.bfloat16)], axis=0
        )

    def whole_history(item):
        return sequence_grads(item[0], item[1], item[2], item[3], item[4], w_query, w_key, w_value)

    def one_history(item):
        return lax.cond(item[4] <= half_span, short_history, whole_history, item)

    result = lax.map(one_history, (query, key_rows, value, grad_heads, lengths))
    return result.reshape(history_count * SEQ_LEN, width)


def onehot_sum(row_count, tile_values, tile_rows, block_rows, initial):
    width = tile_values.shape[-1]
    flat_values = tile_values.reshape(-1, width)
    flat_rows = tile_rows.reshape(-1)
    step_count = flat_rows.shape[0] // block_rows
    target = lax.broadcasted_iota(jnp.int32, (row_count, 1), 0)

    def add_block(accum, item):
        onehot = (target == item[1][None, :]).astype(jnp.bfloat16)
        return (accum + jnp.dot(onehot, item[0], preferred_element_type=jnp.float32), None)

    blocks = (
        flat_values.reshape(step_count, block_rows, width),
        flat_rows.reshape(step_count, block_rows),
    )
    accum, unused = lax.scan(add_block, initial, blocks)
    return accum


def on_device(embeds, out_grad, w_query, w_key, w_value, lengths, item_rows, tile_owner):
    live_total = lax.psum(jnp.sum(lengths.astype(jnp.float32)), ("group", "batch"))
    device_count = lax.axis_size("group") * lax.axis_size("batch")
    scale_factor = embeds.shape[0] * device_count / live_total
    token_grad = token_grads(embeds, out_grad, w_query, w_key, w_value, lengths)
    width = token_grad.shape[1]
    ranking = jnp.argsort(tile_owner, stable=True)
    tile_values = token_grad.reshape(-1, TILE, width)[ranking]
    tile_rows = item_rows.reshape(-1, TILE)[ranking]
    got_values, got_rows = (
        lax.all_to_all(tile_values, "group", split_axis=0, concat_axis=0, tiled=True),
        lax.all_to_all(tile_rows, "group", split_axis=0, concat_axis=0, tiled=True),
    )
    empty_rows = jnp.zeros((ROWS_DEV * lax.axis_size("batch"), width), jnp.float32)
    table = lax.psum_scatter(
        onehot_sum(ROWS_DEV * lax.axis_size("batch"), got_values, got_rows, 4 * TILE, empty_rows),
        "batch",
        scatter_dimension=0,
        tiled=True,
    )
    return scale_factor * table


def solution(mesh):
    in_specs = (
        P(("group", "batch"), None),
        P(("group", "batch"), None),
        P(),
        P(),
        P(),
        P(("group", "batch")),
        P(("group", "batch")),
        P(("group", "batch")),
    )
    out_specs = P(("group", "batch"), None)
    return jax.shard_map(
        on_device, mesh=mesh, in_specs=in_specs, out_specs=out_specs, check_vma=False
    )
```

profile of v0, /device:TPU:0, one launch (start us, length us, event | category | flops | bytes accessed | tf_op | source)
XLA Modules:
  0.0 158.3 jit_solution(10579940593462021619)
XLA Ops:
  6.5 2.0 %sort.17 = (s32[16]{0:T(128)}, s32[16]{0:T(128)S(1)}) sort(s32[16]{0:T(128)} %param.21, s32[16]{0:T(128)S(1)} %iota.48), dimensions={0}, to_apply=%region_6.7 | sort | flops 64 | bytes 256 | tf_op jit(solution)/shard_map/jit(argsort)/sort | solution.py:115
  8.5 1.8 %gather_fusion = s32[16,128]{1,0:T(8,128)} fusion(s32[16,128]{1,0:T(8,128)} %bitcast.105, s32[1024]{0:T(1024)S(1)} %pad_clamp_fusion), kind=kCustom, calls=%fused_computation | custom fusion | bytes 16448 | tf_op jit(solution)/shard_map/gather | solution.py:117
  10.4 6.3 %all-to-all-start = ((s32[4,4,128]{2,1,0:T(4,128)}), s32[4,4,128]{2,1,0:T(4,128)S(1)}, u32[]{:S(2)}, u32[]{:S(2)}) async-start(s32[4,4,128]{2,1,0:T(4,128)} %bitcast.20), calls=%async_computation | async-start | bytes 16384 | tf_op jit(solution)/shard_map/all_to_all | solution.py:120
  16.7 2.2 %reshape.79 = bf16[4,512,2,128]{3,2,1,0:T(2,128)(2,1)} reshape(bf16[2048,256]{1,0:T(8,128)(2,1)} %param.15) | data formatting | bytes 2097152 | tf_op jit(solution)/shard_map/reshape | solution.py:62
  18.9 0.4 convolution_convert_fusion.4
  19.4 0.3 reshape.77
  19.8 0.4 convolution_convert_fusion.3
  20.3 1.1 reshape.78
  21.4 0.4 convolution_convert_fusion.2
  21.8 1.1 reshape.80
  23.0 34.3 %while.21 = (s32[]{:T(128)}, bf16[4,512,256]{2,1,0:T(8,128)(2,1)}, s32[4]{0:T(128)S(1)}, bf16[4,512,2,128]{3,2,1,0:T(2,128)(2,1)S(1)}, bf16[4,512,2,128]{3,2,1,0...) while((s32[]{:T(128)}, bf16[4,512,256]{2,1,0:T(8,128)(2,1)}, ...), condition=%wide.region_5.6_spmd, body=%wide.region_2.5_spmd.sunk | while | flops 883687936 | bytes 23463240 | solution.py:86
  23.0 0.6 dynamic_slice.43
  24.3 1.4 constant_dynamic-slice_fusion.8
  25.8 1.3 constant_dynamic-slice_fusion.9
  27.2 3.6 %conditional.2 = (bf16[1,512,256]{2,1,0:T(8,128)(2,1)S(1)}) conditional(s32[]{:T(128)} %convert_element_type.105, (bf16[512,2,128]{2,0,1:T(8,128)(2,1)S(1)}, bf16[512,2,128]{2,0,1:T(8,128)(2,1)S(1)}, s32[]{:T(128)}, bf16[512,2,128]{2,0,1:T(8,128)(2,1)S(1)}, bf16[512,2,128]{2,0,1:T(8,128)(2,1)S(1)}, /*index=5*/bf16[256,256]{1,0:T(8,128)(2,1)S(1)}, ...), branch_computations={%region_3.3_spmd, %region_4.4_spmd} | conditional | flops 883687936 | bytes 18744356 | solution.py:84
  28.0 0.7 iota_compare_fusion.3
  29.0 0.3 fusion.12
  29.3 0.3 convolution_convert_fusion.1
  29.9 0.2 fusion.13
  30.3 0.2 convolution_add_fusion.3
  30.8 0.7 constant_dynamic-update-slice_fusion.2
  31.6 0.6 dynamic_slice.43
  32.9 1.4 constant_dynamic-slice_fusion.8
  34.4 1.3 constant_dynamic-slice_fusion.9
  35.8 3.6 %conditional.2 = (bf16[1,512,256]{2,1,0:T(8,128)(2,1)S(1)}) conditional(s32[]{:T(128)} %convert_element_type.105, (bf16[512,2,128]{2,0,1:T(8,128)(2,1)S(1)}, bf16[512,2,128]{2,0,1:T(8,128)(2,1)S(1)}, s32[]{:T(128)}, bf16[512,2,128]{2,0,1:T(8,128)(2,1)S(1)}, bf16[512,2,128]{2,0,1:T(8,128)(2,1)S(1)}, /*index=5*/bf16[256,256]{1,0:T(8,128)(2,1)S(1)}, ...), branch_computations={%region_3.3_spmd, %region_4.4_spmd} | conditional | flops 883687936 | bytes 18744356 | solution.py:84
  36.5 0.7 iota_compare_fusion.3
  37.6 0.3 fusion.12
  37.9 0.3 convolution_convert_fusion.1
  38.4 0.2 fusion.13
  38.9 0.2 convolution_add_fusion.3
  39.4 0.7 constant_dynamic-update-slice_fusion.2
  40.1 0.6 dynamic_slice.43
  41.5 1.4 constant_dynamic-slice_fusion.8
  43.0 1.3 constant_dynamic-slice_fusion.9
  44.4 3.6 %conditional.2 = (bf16[1,512,256]{2,1,0:T(8,128)(2,1)S(1)}) conditional(s32[]{:T(128)} %convert_element_type.105, (bf16[512,2,128]{2,0,1:T(8,128)(2,1)S(1)}, bf16[512,2,128]{2,0,1:T(8,128)(2,1)S(1)}, s32[]{:T(128)}, bf16[512,2,128]{2,0,1:T(8,128)(2,1)S(1)}, bf16[512,2,128]{2,0,1:T(8,128)(2,1)S(1)}, /*index=5*/bf16[256,256]{1,0:T(8,128)(2,1)S(1)}, ...), branch_computations={%region_3.3_spmd, %region_4.4_spmd} | conditional | flops 883687936 | bytes 18744356 | solution.py:84
  45.1 0.7 iota_compare_fusion.3
  46.2 0.3 fusion.12
  46.5 0.3 convolution_convert_fusion.1
  47.0 0.2 fusion.13
  47.5 0.2 convolution_add_fusion.3
  48.0 0.7 constant_dynamic-update-slice_fusion.2
  48.7 0.6 dynamic_slice.43
  50.1 1.4 constant_dynamic-slice_fusion.8
  51.5 1.3 constant_dynamic-slice_fusion.9
  53.0 3.6 %conditional.2 = (bf16[1,512,256]{2,1,0:T(8,128)(2,1)S(1)}) conditional(s32[]{:T(128)} %convert_element_type.105, (bf16[512,2,128]{2,0,1:T(8,128)(2,1)S(1)}, bf16[512,2,128]{2,0,1:T(8,128)(2,1)S(1)}, s32[]{:T(128)}, bf16[512,2,128]{2,0,1:T(8,128)(2,1)S(1)}, bf16[512,2,128]{2,0,1:T(8,128)(2,1)S(1)}, /*index=5*/bf16[256,256]{1,0:T(8,128)(2,1)S(1)}, ...), branch_computations={%region_3.3_spmd, %region_4.4_spmd} | conditional | flops 883687936 | bytes 18744356 | solution.py:84
  53.7 0.7 iota_compare_fusion.3
  54.7 0.3 fusion.12
  55.1 0.3 convolution_convert_fusion.1
  55.6 0.2 fusion.13
  56.1 0.2 convolution_add_fusion.3
  56.6 0.7 constant_dynamic-update-slice_fusion.2
  57.3 2.9 %gather_fusion.1 = bf16[16,128,256]{2,1,0:T(8,128)(2,1)} fusion(bf16[16,128,256]{2,1,0:T(8,128)(2,1)} %bitcast.104, s32[1024]{0:T(1024)S(1)} %pad_clamp_fusion), kind=kCustom, calls=%fused_computation.1 | custom fusion | bytes 2097216 | tf_op jit(solution)/shard_map/gather | solution.py:116
  60.2 5.1 %all-to-all-start.1 = ((bf16[16,128,256]{2,1,0:T(8,128)(2,1)}), bf16[16,128,256]{2,1,0:T(8,128)(2,1)}, u32[]{:S(2)}, u32[]{:S(2)}) async-start(bf16[16,128,256]{2,1,0:T(8,128)(2,1)} %gather_fusion.1), calls=%async_computation.1 | async-start | bytes 2097152 | tf_op jit(solution)/shard_map/all_to_all | solution.py:119
  65.3 25.3 %all-to-all-done.1 = bf16[16,128,256]{2,1,0:T(8,128)(2,1)} async-done(((bf16[16,128,256]{2,1,0:T(8,128)(2,1)}), bf16[16,128,256]{2,1,0:T(8,128)(2,1)}, u32[]{:S(2)}, u32[]{:S(2)}) %all-to-all-start.1) | async-done | bytes 1048608 | tf_op jit(solution)/shard_map/all_to_all | solution.py:119
  90.5 9.5 %while.22 = (s32[]{:T(128)}, f32[2048,256]{1,0:T(8,128)S(1)}, s32[4,512]{1,0:T(4,128)S(1)}, bf16[4,512,256]{2,1,0:T(8,128)(2,1)}, s32[]{:T(128)}, /*index=5*/s32[]{:T(128)}) while((s32[]{:T(128)}, f32[2048,256]{1,0:T(8,128)S(1)}, s32[4,512]{1,0:T(4,128)S(1)}, bf16[4,512,256]{2,1,0:T(8,128)(2,1)}, s32[]{:T(128)}, ...), condition=%wide.region_8.9_spmd.clone, body=%wide.region_7.8_spmd.clone.sunk | while | flops 538968064 | bytes 4462687 | solution.py:105
  90.5 2.3 %fusion.67 = f32[2048,256]{1,0:T(8,128)S(1)} fusion(f32[2048,256]{1,0:T(8,128)S(1)} %get-tuple-element.362, s32[512]{0:T(512)S(1)} %bitcast.106, pred[]{:T(512)S(6)} %compare.8, bf16[4,512,256]{2,1,0:T(8,128)(2,1)} %get-tuple-element.370, s32[]{:T(128)S(6)} %copy.74), kind=kOutput, calls=%fused_computation.60.clone.1 | convolution fusion | flops 538968064 | bytes 4458501 | tf_op jit(solution)/shard_map/while/body/eval_jaxpr/dot_general | solution.py:99
  92.9 2.3 %fusion.67 = f32[2048,256]{1,0:T(8,128)S(1)} fusion(f32[2048,256]{1,0:T(8,128)S(1)} %get-tuple-element.362, s32[512]{0:T(512)S(1)} %bitcast.106, pred[]{:T(512)S(6)} %compare.8, bf16[4,512,256]{2,1,0:T(8,128)(2,1)} %get-tuple-element.370, s32[]{:T(128)S(6)} %copy.74), kind=kOutput, calls=%fused_computation.60.clone.1 | convolution fusion | flops 538968064 | bytes 4458501 | tf_op jit(solution)/shard_map/while/body/eval_jaxpr/dot_general | solution.py:99
  95.3 2.3 %fusion.67 = f32[2048,256]{1,0:T(8,128)S(1)} fusion(f32[2048,256]{1,0:T(8,128)S(1)} %get-tuple-element.362, s32[512]{0:T(512)S(1)} %bitcast.106, pred[]{:T(512)S(6)} %compare.8, bf16[4,512,256]{2,1,0:T(8,128)(2,1)} %get-tuple-element.370, s32[]{:T(128)S(6)} %copy.74), kind=kOutput, calls=%fused_computation.60.clone.1 | convolution fusion | flops 538968064 | bytes 4458501 | tf_op jit(solution)/shard_map/while/body/eval_jaxpr/dot_general | solution.py:99
  97.7 2.3 %fusion.67 = f32[2048,256]{1,0:T(8,128)S(1)} fusion(f32[2048,256]{1,0:T(8,128)S(1)} %get-tuple-element.362, s32[512]{0:T(512)S(1)} %bitcast.106, pred[]{:T(512)S(6)} %compare.8, bf16[4,512,256]{2,1,0:T(8,128)(2,1)} %get-tuple-element.370, s32[]{:T(128)S(6)} %copy.74), kind=kOutput, calls=%fused_computation.60.clone.1 | convolution fusion | flops 538968064 | bytes 4458501 | tf_op jit(solution)/shard_map/while/body/eval_jaxpr/dot_general | solution.py:99
  100.0 1.3 copy-done.1
  101.4 0.6 convert_reduce_fusion
  102.0 45.7 %psum.7 = f32[]{:T(128)} all-reduce(f32[]{:T(128)} %convert_reduce_fusion), channel_id=1, replica_groups=mesh['group'=4,'batch'=8] {'group','batch'}, use_global_device_ids=true, to_apply=%region_1.0 | all-reduce | flops 1 | bytes 8 | tf_op jit(solution)/shard_map/psum | solution.py:110
  148.4 1.4 reduce-scatter.2.cloned.1.call-done
  149.8 1.7 %broadcast_multiply_fusion = f32[256,256]{1,0:T(8,128)} fusion(f32[256,256]{1,0:T(8,128)} %reduce-scatter.2.cloned.1.call-done, f32[]{:T(128)S(6)} %div.21), kind=kLoop, calls=%fused_computation.69 | loop fusion | flops 65536 | bytes 524292 | tf_op jit(solution)/shard_map/mul | solution.py:129
  (64 shorter events, 5.0 us)
Async XLA Ops:
  6.5 12.4 %copy-start = (bf16[2048,256]{1,0:T(8,128)(2,1)S(1)}, bf16[2048,256]{1,0:T(8,128)(2,1)}, u32[]{:S(2)}) copy-start(bf16[2048,256]{1,0:T(8,128)(2,1)} %param.14) | copy-start | bytes 3145732
  6.5 12.4 %copy-start.3 = (bf16[256,256]{1,0:T(8,128)(2,1)S(1)}, bf16[256,256]{1,0:T(8,128)(2,1)}, u32[]{:S(2)}) copy-start(bf16[256,256]{1,0:T(8,128)(2,1)} %param.16) | copy-start | bytes 393220
  10.4 49.8 %all-to-all-start = ((s32[4,4,128]{2,1,0:T(4,128)}), s32[4,4,128]{2,1,0:T(4,128)S(1)}, u32[]{:S(2)}, u32[]{:S(2)}) async-start(s32[4,4,128]{2,1,0:T(4,128)} %bitcast.20), calls=%async_computation | async-start | bytes 16384 | tf_op jit(solution)/shard_map/all_to_all | solution.py:120
  18.9 0.9 copy-start.4
  19.8 1.6 copy-start.2
  21.4 1.6 %copy-start.5 = (s32[4]{0:T(128)S(1)}, s32[4]{0:T(128)}, u32[]{:S(2)}) copy-start(s32[4]{0:T(128)} %param.19) | copy-start | bytes 52
  60.2 30.4 %all-to-all-start.1 = ((bf16[16,128,256]{2,1,0:T(8,128)(2,1)}), bf16[16,128,256]{2,1,0:T(8,128)(2,1)}, u32[]{:S(2)}, u32[]{:S(2)}) async-start(bf16[16,128,256]{2,1,0:T(8,128)(2,1)} %gather_fusion.1), calls=%async_computation.1 | async-start | bytes 2097152 | tf_op jit(solution)/shard_map/all_to_all | solution.py:119
  65.3 84.6 %reduce-scatter.2.cloned.1.call-start = ((), (), s32[]{:S(2)}) async-start(), calls=%async_computation.3 | async-start | bytes 2359296 | tf_op jit(solution)/shard_map/reduce_scatter | solution.py:123
  100.0 1.3 copy-start.1
Sparse Core Ops, SparseCore 0:
  101.5 48.2 reduce-scatter.1
where the time goes:
time: 159 us; the launch traced here: 158 us
  blocking collectives  45.7 us (29%)
  local copies, waits for them, and re-layouts  28 us (18%)
  waiting for transfers between devices  26.7 us (17%)
  matrix products  18.7 us (12%)
  between operations  14.1 us (9%)
  starting transfers between devices  11.4 us (7%)
  other arithmetic  7.41 us (5%)
  loops' own time  6.25 us (4%)
    psum x1, blocking collectives, on_device(): lax.psum(jnp.sum(lengths.astype(jnp.float32)), ('group', 'batch'))  45.7 us
    all_to_all x1, waiting for transfers between devices, on_device(): lax.all_to_all(tile_values, 'group', split_axis=0, concat_axis=0, tiled=T...  25.3 us
    dynamic_slice x28, local copies, waits for them, and re-layouts, token_grads(): result = lax.map(one_history, (query, key_rows, value, grad_heads, lengths))  14 us
    dot_general x4, matrix products, add_block(): jnp.dot(onehot, item[0], preferred_element_type=jnp.float32)  9.34 us
    all_to_all x1, starting transfers between devices, on_device(): lax.all_to_all(tile_rows, 'group', split_axis=0, concat_axis=0, tiled=True)  6.35 us
    all_to_all x1, starting transfers between devices, on_device(): lax.all_to_all(tile_values, 'group', split_axis=0, concat_axis=0, tiled=T...  5.09 us
    another operation x4, loops' own time, one_history(): return lax.cond(item[4] <= half_span, short_history, whole_history, item)  3.22 us
  transfers between devices with their start and end apart: 3, of which 2 were waited for; matrix products, arithmetic and copies ran while one was open for 24% of the time, Pallas kernels for 0%

commit v1 on v0

--- a/solution.py
+++ b/solution.py
@@ -8,6 +8,30 @@
 TILE = 128
 SEQ_LEN = 512
 ROWS_DEV = 256
+
+
+def in_blocks(x, dim, length):
+    dims = x.shape
+    parts = x.reshape(*dims[:dim], length, dims[dim] // length, *dims[dim + 1 :])
+    return jnp.moveaxis(parts, dim, 0)
+
+
+def laid_out(blocks, dim):
+    shape = list(blocks.shape[1:])
+    shape[dim] *= blocks.shape[0]
+    return jnp.moveaxis(blocks, 0, dim).reshape(shape)
+
+
+def rotated_exchange(x, axis, split_dim, concat_dim):
+    size, mine = (lax.axis_size(axis), lax.axis_index(axis))
+    tiles = in_blocks(x, split_dim, size)
+    filled = tiles
+    for step in range(1, size):
+        target, source = ((mine + step) % size, (mine - step) % size)
+        sent = lax.dynamic_index_in_dim(tiles, target, 0)
+        theirs = lax.ppermute(sent, axis, [(i, (i + step) % size) for i in range(size)])
+        filled = lax.dynamic_update_slice_in_dim(filled, theirs, source, axis=0)
+    return laid_out(filled, concat_dim)
 
 
 def sequence_grads(query, key_rows, value, grad_out, count, w_query, w_key, w_value):
@@ -116,7 +140,7 @@
     tile_values = token_grad.reshape(-1, TILE, width)[ranking]
     tile_rows = item_rows.reshape(-1, TILE)[ranking]
     got_values, got_rows = (
-        lax.all_to_all(tile_values, "group", split_axis=0, concat_axis=0, tiled=True),
+        rotated_exchange(tile_values, "group", 0, 0),
         lax.all_to_all(tile_rows, "group", split_axis=0, concat_axis=0, tiled=True),
     )
     empty_rows = jnp.zeros((ROWS_DEV * lax.axis_size("batch"), width), jnp.float32)

time: 159 us -> 154 us (0.969)
  waiting for transfers between devices: 26.7 us -> 21.1 us
  starting transfers between devices: 11.4 us -> 8.76 us
  local copies, waits for them, and re-layouts: 28 us -> 30 us
  blocking collectives: 45.7 us -> 47.6 us
    all_to_all x1 -> x0, waiting for transfers between devices: 25.3 us -> none  [on_device(): lax.all_to_all(tile_values, 'group', split_axis=0, concat_axis=0, tiled=T...]
    all_to_all x1, waiting for transfers between devices: 0.01 us -> 12.1 us  [on_device(): lax.all_to_all(tile_rows, 'group', split_axis=0, concat_axis=0, tiled=True)]
    ppermute x0 -> x3, waiting for transfers between devices: none -> 8.32 us  [rotated_exchange(): lax.ppermute(sent, axis, [(i, (i + step) % size) for i in range(size)])]
    ppermute x0 -> x3, starting transfers between devices: none -> 5.19 us  [rotated_exchange(): lax.ppermute(sent, axis, [(i, (i + step) % size) for i in range(size)])]
    all_to_all x1 -> x0, starting transfers between devices: 5.09 us -> none  [on_device(): lax.all_to_all(tile_values, 'group', split_axis=0, concat_axis=0, tiled=T...]
    dynamic_update_slice x0 -> x2, local copies, waits for them, and re-layouts: none -> 3.33 us  [rotated_exchange(): filled = lax.dynamic_update_slice_in_dim(filled, theirs, source, axis=0)]
    all_to_all x1, starting transfers between devices: 6.35 us -> 3.57 us  [on_device(): lax.all_to_all(tile_rows, 'group', split_axis=0, concat_axis=0, tiled=True)]
    psum x1, blocking collectives: 45.7 us -> 47.6 us  [on_device(): lax.psum(jnp.sum(lengths.astype(jnp.float32)), ('group', 'batch'))]
  transfers between devices with their start and end apart: 3 -> 5, of which waited for: 2 -> 3; matrix products, arithmetic and copies ran while one was open for 24% -> 2% of each run, Pallas kernels for 0% -> 0%
where the time goes in v1:
time: 154 us
  blocking collectives  47.6 us (31%)
  local copies, waits for them, and re-layouts  30 us (19%)
  waiting for transfers between devices  21.1 us (14%)
  matrix products  18.6 us (12%)
  between operations  14.2 us (9%)
  starting transfers between devices  8.76 us (6%)
  other arithmetic  7.28 us (5%)
  loops' own time  6.01 us (4%)
    psum x1, blocking collectives, on_device(): lax.psum(jnp.sum(lengths.astype(jnp.float32)), ('group', 'batch'))  47.6 us
    dynamic_slice x28, local copies, waits for them, and re-layouts, token_grads(): result = lax.map(one_history, (query, key_rows, value, grad_heads, lengths))  13.8 us
    all_to_all x1, waiting for transfers between devices, on_device(): lax.all_to_all(tile_rows, 'group', split_axis=0, concat_axis=0, tiled=True)  12.1 us
    dot_general x4, matrix products, add_block(): jnp.dot(onehot, item[0], preferred_element_type=jnp.float32)  9.34 us
    ppermute x3, waiting for transfers between devices, rotated_exchange(): lax.ppermute(sent, axis, [(i, (i + step) % size) for i in range(size)])  8.32 us
    ppermute x3, starting transfers between devices, rotated_exchange(): lax.ppermute(sent, axis, [(i, (i + step) % size) for i in range(size)])  5.19 us
    all_to_all x1, starting transfers between devices, on_device(): lax.all_to_all(tile_rows, 'group', split_axis=0, concat_axis=0, tiled=True)  3.57 us
    reshape x3, local copies, waits for them, and re-layouts, project(): return jnp.dot(embeds, weight_matrix, preferred_element_type=jnp.float32)...  3.42 us
  transfers between devices with their start and end apart: 5, of which 3 were waited for; matrix products, arithmetic and copies ran while one was open for 2% of the time, Pallas kernels for 0%

profile of v1, /device:TPU:0, one launch (start us, length us, event | category | flops | bytes accessed | tf_op | source)
XLA Modules:
  0.0 153.6 jit_solution(10721177313169218433)
XLA Ops:
  6.5 2.0 %sort.17 = (s32[16]{0:T(128)}, s32[16]{0:T(128)S(1)}) sort(s32[16]{0:T(128)} %param.21, s32[16]{0:T(128)S(1)} %iota.48), dimensions={0}, to_apply=%region_6.7 | sort | flops 64 | bytes 256 | tf_op jit(solution)/shard_map/jit(argsort)/sort | solution.py:139
  8.5 1.3 reshape.82
  9.9 0.4 convolution_convert_fusion.4
  10.4 1.1 reshape.80
  11.5 0.4 convolution_convert_fusion.3
  11.9 1.2 reshape.81
  13.1 0.4 convolution_convert_fusion.2
  13.5 1.1 reshape.83
  14.7 33.6 %while.21 = (s32[]{:T(128)}, bf16[4,512,256]{2,1,0:T(8,128)(2,1)}, s32[4]{0:T(128)S(1)}, bf16[4,512,2,128]{3,2,1,0:T(2,128)(2,1)}, bf16[4,512,2,128]{3,2,1,0:T(2...) while((s32[]{:T(128)}, bf16[4,512,256]{2,1,0:T(8,128)(2,1)}, ...), condition=%wide.region_5.6_spmd, body=%wide.region_2.5_spmd.sunk | while | flops 883687936 | bytes 23463240 | solution.py:110
  14.7 0.6 dynamic_slice.59
  15.9 1.3 constant_dynamic-slice_fusion.11
  17.3 1.4 constant_dynamic-slice_fusion.12
  18.8 3.5 %conditional.2 = (bf16[1,512,256]{2,1,0:T(8,128)(2,1)S(1)}) conditional(s32[]{:T(128)} %convert_element_type.105, (bf16[512,2,128]{2,0,1:T(8,128)(2,1)S(1)}, bf16[512,2,128]{2,0,1:T(8,128)(2,1)S(1)}, s32[]{:T(128)}, bf16[512,2,128]{2,0,1:T(8,128)(2,1)S(1)}, bf16[512,2,128]{2,0,1:T(8,128)(2,1)S(1)}, /*index=5*/bf16[256,256]{1,0:T(8,128)(2,1)S(1)}, ...), branch_computations={%region_3.3_spmd, %region_4.4_spmd} | conditional | flops 883687936 | bytes 18744356 | solution.py:108
  19.5 0.7 iota_compare_fusion.3
  20.5 0.3 fusion.12
  20.8 0.3 convolution_convert_fusion.1
  21.4 0.2 fusion.13
  22.4 0.7 constant_dynamic-update-slice_fusion.5
  23.1 0.6 dynamic_slice.59
  24.3 1.3 constant_dynamic-slice_fusion.11
  25.7 1.4 constant_dynamic-slice_fusion.12
  27.2 3.5 %conditional.2 = (bf16[1,512,256]{2,1,0:T(8,128)(2,1)S(1)}) conditional(s32[]{:T(128)} %convert_element_type.105, (bf16[512,2,128]{2,0,1:T(8,128)(2,1)S(1)}, bf16[512,2,128]{2,0,1:T(8,128)(2,1)S(1)}, s32[]{:T(128)}, bf16[512,2,128]{2,0,1:T(8,128)(2,1)S(1)}, bf16[512,2,128]{2,0,1:T(8,128)(2,1)S(1)}, /*index=5*/bf16[256,256]{1,0:T(8,128)(2,1)S(1)}, ...), branch_computations={%region_3.3_spmd, %region_4.4_spmd} | conditional | flops 883687936 | bytes 18744356 | solution.py:108
  27.9 0.7 iota_compare_fusion.3
  28.9 0.3 fusion.12
  29.3 0.3 convolution_convert_fusion.1
  29.8 0.2 fusion.13
  30.8 0.7 constant_dynamic-update-slice_fusion.5
  31.5 0.6 dynamic_slice.59
  32.7 1.3 constant_dynamic-slice_fusion.11
  34.1 1.4 constant_dynamic-slice_fusion.12
  35.6 3.5 %conditional.2 = (bf16[1,512,256]{2,1,0:T(8,128)(2,1)S(1)}) conditional(s32[]{:T(128)} %convert_element_type.105, (bf16[512,2,128]{2,0,1:T(8,128)(2,1)S(1)}, bf16[512,2,128]{2,0,1:T(8,128)(2,1)S(1)}, s32[]{:T(128)}, bf16[512,2,128]{2,0,1:T(8,128)(2,1)S(1)}, bf16[512,2,128]{2,0,1:T(8,128)(2,1)S(1)}, /*index=5*/bf16[256,256]{1,0:T(8,128)(2,1)S(1)}, ...), branch_computations={%region_3.3_spmd, %region_4.4_spmd} | conditional | flops 883687936 | bytes 18744356 | solution.py:108
  36.3 0.7 iota_compare_fusion.3
  37.3 0.3 fusion.12
  37.7 0.3 convolution_convert_fusion.1
  39.2 0.7 constant_dynamic-update-slice_fusion.5
  39.9 0.6 dynamic_slice.59
  41.1 1.3 constant_dynamic-slice_fusion.11
  42.5 1.4 constant_dynamic-slice_fusion.12
  44.0 3.5 %conditional.2 = (bf16[1,512,256]{2,1,0:T(8,128)(2,1)S(1)}) conditional(s32[]{:T(128)} %convert_element_type.105, (bf16[512,2,128]{2,0,1:T(8,128)(2,1)S(1)}, bf16[512,2,128]{2,0,1:T(8,128)(2,1)S(1)}, s32[]{:T(128)}, bf16[512,2,128]{2,0,1:T(8,128)(2,1)S(1)}, bf16[512,2,128]{2,0,1:T(8,128)(2,1)S(1)}, /*index=5*/bf16[256,256]{1,0:T(8,128)(2,1)S(1)}, ...), branch_computations={%region_3.3_spmd, %region_4.4_spmd} | conditional | flops 883687936 | bytes 18744356 | solution.py:108
  44.7 0.7 iota_compare_fusion.3
  45.7 0.3 fusion.12
  46.1 0.3 convolution_convert_fusion.1
  47.6 0.7 constant_dynamic-update-slice_fusion.5
  48.3 1.9 %gather_fusion.1 = bf16[16,128,256]{2,1,0:T(8,128)(2,1)S(1)} fusion(bf16[16,128,256]{2,1,0:T(8,128)(2,1)} %bitcast.108, s32[1024]{0:T(1024)S(1)} %pad_clamp_fusion), kind=kCustom, calls=%fused_computation.1 | custom fusion | bytes 2097216 | tf_op jit(solution)/shard_map/gather | solution.py:140
  50.2 3.1 %collective-permute-start = (bf16[1,4,128,256]{3,2,1,0:T(8,128)(2,1)S(1)}, bf16[1,4,128,256]{3,2,1,0:T(8,128)(2,1)S(1)}, u32[]{:S(2)}, u32[]{:S(2)}) collective-permute-start(bf16[1,4,128,256]{3,2,1,0:T(8,128)(2,1)S(1)} %constant_dynamic-slice_fusion.7), channel_id=1, source_target_pairs={{0,8},{8,16},{16,24},{24,0},{1,9},{9,17},{17,25},{25,1},{2,10},{10... | collective-permute-start | bytes 786440 | tf_op jit(solution)/shard_map/ppermute | solution.py:32
  53.3 8.3 %collective-permute-done = bf16[1,4,128,256]{3,2,1,0:T(8,128)(2,1)S(1)} collective-permute-done((bf16[1,4,128,256]{3,2,1,0:T(8,128)(2,1)S(1)}, bf16[1,4,128,256]{3,2,1,0:T(8,128)(2,1)S(1)}, u32[]{:S(2)}, u32[]{:S(2)}) %collective-permute-start) | collective-permute-done | bytes 262176 | tf_op jit(solution)/shard_map/ppermute | solution.py:32
  61.6 0.8 constant_dynamic-slice_fusion.5
  62.4 0.7 collective-permute-start.1
  63.1 1.4 collective-permute-start.2
  64.5 1.1 gather_fusion
  65.6 3.6 %all-to-all-start = ((s32[4,4,128]{2,1,0:T(4,128)}), s32[4,4,128]{2,1,0:T(4,128)S(1)}, u32[]{:S(2)}, u32[]{:S(2)}) async-start(s32[4,4,128]{2,1,0:T(4,128)} %bitcast.20), calls=%async_computation | async-start | bytes 16384 | tf_op jit(solution)/shard_map/all_to_all | solution.py:144
  69.2 12.1 %all-to-all-done = s32[4,4,128]{2,1,0:T(4,128)S(1)} async-done(((s32[4,4,128]{2,1,0:T(4,128)}), s32[4,4,128]{2,1,0:T(4,128)S(1)}, u32[]{:S(2)}, u32[]{:S(2)}) %all-to-all-start) | async-done | bytes 8224 | tf_op jit(solution)/shard_map/all_to_all | solution.py:144
  81.3 1.7 %constant_dynamic-update-slice_fusion.2 = bf16[4,4,128,256]{3,2,1,0:T(8,128)(2,1)} fusion(bf16[4,4,128,256]{3,2,1,0:T(8,128)(2,1)} %copy-done.5, bf16[1,4,128,256]{3,2,1,0:T(8,128)(2,1)} %collective-permute-done.1, s32[]{:T(128)S(6)} %select_n.58), kind=kLoop, calls=%fused_computation.75 | loop fusion | bytes 524292 | tf_op jit(solution)/shard_map/dynamic_update_slice | solution.py:33
  83.0 1.7 %constant_dynamic-update-slice_fusion.1 = bf16[4,4,128,256]{3,2,1,0:T(8,128)(2,1)} fusion(bf16[4,4,128,256]{3,2,1,0:T(8,128)(2,1)} %constant_dynamic-update-slice_fusion.2, bf16[1,4,128,256]{3,2,1,0:T(8,128)(2,1)} %collective-permute-done.2, s32[]{:T(128)S(6)} %select_n.62), kind=kLoop, calls=%fused_computation.73 | loop fusion | bytes 524292 | tf_op jit(solution)/shard_map/dynamic_update_slice | solution.py:33
  84.6 9.5 %while.22 = (s32[]{:T(128)}, f32[2048,256]{1,0:T(8,128)S(1)}, s32[4,512]{1,0:T(4,128)S(1)}, bf16[4,512,256]{2,1,0:T(8,128)(2,1)}, s32[]{:T(128)}, /*index=5*/s32[]{:T(128)}) while((s32[]{:T(128)}, f32[2048,256]{1,0:T(8,128)S(1)}, s32[4,512]{1,0:T(4,128)S(1)}, bf16[4,512,256]{2,1,0:T(8,128)(2,1)}, s32[]{:T(128)}, ...), condition=%wide.region_8.9_spmd.clone, body=%wide.region_7.8_spmd.clone.sunk | while | flops 538968064 | bytes 4462687 | solution.py:129
  84.6 2.3 %fusion.67 = f32[2048,256]{1,0:T(8,128)S(1)} fusion(f32[2048,256]{1,0:T(8,128)S(1)} %get-tuple-element.365, s32[512]{0:T(512)S(1)} %bitcast.110, pred[]{:T(512)S(6)} %compare.14, bf16[4,512,256]{2,1,0:T(8,128)(2,1)} %get-tuple-element.373, s32[]{:T(128)S(6)} %copy.77), kind=kOutput, calls=%fused_computation.60.clone.1 | convolution fusion | flops 538968064 | bytes 4458501 | tf_op jit(solution)/shard_map/while/body/eval_jaxpr/dot_general | solution.py:123
  87.0 2.3 %fusion.67 = f32[2048,256]{1,0:T(8,128)S(1)} fusion(f32[2048,256]{1,0:T(8,128)S(1)} %get-tuple-element.365, s32[512]{0:T(512)S(1)} %bitcast.110, pred[]{:T(512)S(6)} %compare.14, bf16[4,512,256]{2,1,0:T(8,128)(2,1)} %get-tuple-element.373, s32[]{:T(128)S(6)} %copy.77), kind=kOutput, calls=%fused_computation.60.clone.1 | convolution fusion | flops 538968064 | bytes 4458501 | tf_op jit(solution)/shard_map/while/body/eval_jaxpr/dot_general | solution.py:123
  89.4 2.3 %fusion.67 = f32[2048,256]{1,0:T(8,128)S(1)} fusion(f32[2048,256]{1,0:T(8,128)S(1)} %get-tuple-element.365, s32[512]{0:T(512)S(1)} %bitcast.110, pred[]{:T(512)S(6)} %compare.14, bf16[4,512,256]{2,1,0:T(8,128)(2,1)} %get-tuple-element.373, s32[]{:T(128)S(6)} %copy.77), kind=kOutput, calls=%fused_computation.60.clone.1 | convolution fusion | flops 538968064 | bytes 4458501 | tf_op jit(solution)/shard_map/while/body/eval_jaxpr/dot_general | solution.py:123
  91.7 2.3 %fusion.67 = f32[2048,256]{1,0:T(8,128)S(1)} fusion(f32[2048,256]{1,0:T(8,128)S(1)} %get-tuple-element.365, s32[512]{0:T(512)S(1)} %bitcast.110, pred[]{:T(512)S(6)} %compare.14, bf16[4,512,256]{2,1,0:T(8,128)(2,1)} %get-tuple-element.373, s32[]{:T(128)S(6)} %copy.77), kind=kOutput, calls=%fused_computation.60.clone.1 | convolution fusion | flops 538968064 | bytes 4458501 | tf_op jit(solution)/shard_map/while/body/eval_jaxpr/dot_general | solution.py:123
  94.1 1.3 copy-done.1
  95.5 0.6 convert_reduce_fusion
  96.1 47.6 %psum.7 = f32[]{:T(128)} all-reduce(f32[]{:T(128)} %convert_reduce_fusion), channel_id=1, replica_groups=mesh['group'=4,'batch'=8] {'group','batch'}, use_global_device_ids=true, to_apply=%region_1.0 | all-reduce | flops 1 | bytes 8 | tf_op jit(solution)/shard_map/psum | solution.py:134
  144.4 0.6 reduce-scatter.2.cloned.1.call-done
  145.0 1.7 %broadcast_multiply_fusion = f32[256,256]{1,0:T(8,128)} fusion(f32[256,256]{1,0:T(8,128)} %reduce-scatter.2.cloned.1.call-done, f32[]{:T(128)S(6)} %div.21), kind=kLoop, calls=%fused_computation.69 | loop fusion | flops 65536 | bytes 524292 | tf_op jit(solution)/shard_map/mul | solution.py:153
  (76 shorter events, 6.2 us)
Async XLA Ops:
  6.5 3.4 %copy-start = (bf16[2048,256]{1,0:T(8,128)(2,1)S(1)}, bf16[2048,256]{1,0:T(8,128)(2,1)}, u32[]{:S(2)}) copy-start(bf16[2048,256]{1,0:T(8,128)(2,1)} %param.14) | copy-start | bytes 3145732
  6.5 3.4 %copy-start.3 = (bf16[256,256]{1,0:T(8,128)(2,1)S(1)}, bf16[256,256]{1,0:T(8,128)(2,1)}, u32[]{:S(2)}) copy-start(bf16[256,256]{1,0:T(8,128)(2,1)} %param.16) | copy-start | bytes 393220
  9.9 1.6 %copy-start.4 = (bf16[256,256]{1,0:T(8,128)(2,1)S(1)}, bf16[256,256]{1,0:T(8,128)(2,1)}, u32[]{:S(2)}) copy-start(bf16[256,256]{1,0:T(8,128)(2,1)} %param.17) | copy-start | bytes 393220
  11.5 1.6 %copy-start.2 = (bf16[256,256]{1,0:T(8,128)(2,1)S(1)}, bf16[256,256]{1,0:T(8,128)(2,1)}, u32[]{:S(2)}) copy-start(bf16[256,256]{1,0:T(8,128)(2,1)} %param.18) | copy-start | bytes 393220
  13.1 1.6 %copy-start.7 = (s32[4]{0:T(128)S(1)}, s32[4]{0:T(128)}, u32[]{:S(2)}) copy-start(s32[4]{0:T(128)} %param.19) | copy-start | bytes 52
  48.3 16.2 %copy-start.6 = (s32[2048]{0:T(1024)S(1)}, s32[2048]{0:T(1024)}, u32[]{:S(2)}) copy-start(s32[2048]{0:T(1024)} %param.20) | copy-start | bytes 24580
  50.2 11.4 %collective-permute-start = (bf16[1,4,128,256]{3,2,1,0:T(8,128)(2,1)S(1)}, bf16[1,4,128,256]{3,2,1,0:T(8,128)(2,1)S(1)}, u32[]{:S(2)}, u32[]{:S(2)}) collective-permute-start(bf16[1,4,128,256]{3,2,1,0:T(8,128)(2,1)S(1)} %constant_dynamic-slice_fusion.7), channel_id=1, source_target_pairs={{0,8},{8,16},{16,24},{24,0},{1,9},{9,17},{17,25},{25,1},{2,10},{10... | collective-permute-start | bytes 786440 | tf_op jit(solution)/shard_map/ppermute | solution.py:32
  62.4 6.8 %copy-start.5 = (bf16[4,4,128,256]{3,2,1,0:T(8,128)(2,1)}, bf16[4,4,128,256]{3,2,1,0:T(8,128)(2,1)S(1)}, u32[]{:S(2)}) copy-start(bf16[4,4,128,256]{3,2,1,0:T(8,128)(2,1)S(1)} %get-tuple-element.227) | copy-start | bytes 3145732
  62.4 18.9 %collective-permute-start.1 = (bf16[1,4,128,256]{3,2,1,0:T(8,128)(2,1)}, bf16[1,4,128,256]{3,2,1,0:T(8,128)(2,1)}, u32[]{:S(2)}, u32[]{:S(2)}) collective-permute-start(bf16[1,4,128,256]{3,2,1,0:T(8,128)(2,1)} %get-tuple-element.226), channel_id=1, source_target_pairs={{0,16},{8,24},{16,0},{24,8},{1,17},{9,25},{17,1},{25,9},{2,18},{10... | collective-permute-start | bytes 786440 | tf_op jit(solution)/shard_map/ppermute | solution.py:32
  63.1 19.9 %collective-permute-start.2 = (bf16[1,4,128,256]{3,2,1,0:T(8,128)(2,1)S(1)}, bf16[1,4,128,256]{3,2,1,0:T(8,128)(2,1)}, u32[]{:S(2)}, u32[]{:S(2)}) collective-permute-start(bf16[1,4,128,256]{3,2,1,0:T(8,128)(2,1)S(1)} %get-tuple-element.225), channel_id=1, source_target_pairs={{0,24},{8,0},{16,8},{24,16},{1,25},{9,1},{17,9},{25,17},{2,26},{10... | collective-permute-start | bytes 786440 | tf_op jit(solution)/shard_map/ppermute | solution.py:32
  65.6 15.7 %all-to-all-start = ((s32[4,4,128]{2,1,0:T(4,128)}), s32[4,4,128]{2,1,0:T(4,128)S(1)}, u32[]{:S(2)}, u32[]{:S(2)}) async-start(s32[4,4,128]{2,1,0:T(4,128)} %bitcast.20), calls=%async_computation | async-start | bytes 16384 | tf_op jit(solution)/shard_map/all_to_all | solution.py:144
  69.2 75.9 %reduce-scatter.2.cloned.1.call-start = ((), (), s32[]{:S(2)}) async-start(), calls=%async_computation.2 | async-start | bytes 2359296 | tf_op jit(solution)/shard_map/reduce_scatter | solution.py:147
  94.1 1.3 copy-start.1
Sparse Core Ops, SparseCore 0:
  95.6 49.3 reduce-scatter.1
